TPU v7x, 32 devices: a whole 2x2x4 slice. The times are simulated.
32 devices in a mesh: ep: 8 (over y, x, core), tp: 4 (over z).
Axes of the slice: x: 2, y: 2, z: 4, core: 2. Of those that a mesh axis runs over, the one named last changes fastest.
Arguments:
- tokens: bfloat16 [256, 4096], P('ep', 'tp'), may hold values from -6 to 6
- norm_gains: float32 [2, 4096], replicated, may hold values from 0.1 to 1.9
- router: bfloat16 [2, 4096, 16], replicated, as said below
- w_gate: bfloat16 [2, 16, 4096, 768], P(None, 'ep', None, 'tp'), may hold values from -0.09375 to 0.09375
- w_up: bfloat16 [2, 16, 4096, 768], P(None, 'ep', None, 'tp'), may hold values from -0.09375 to 0.09375
- w_down: bfloat16 [2, 16, 768, 4096], P(None, 'ep', 'tp'), may hold values from -0.21875 to 0.21875
- expert_ids: int32 [2, 256, 8], P(None, 'ep'), may hold values from 0 to 15, all different within a row; in each aligned block of 32 rows (0 to 31, 32 to 63, ...) at most 32 rows name the same one
Outputs:
- hidden_out: bfloat16 [256, 4096], P('ep', 'tp')
Inputs may be any that keep to these rules, and one draw needn't show every extreme that they name: `expert_ids`: each entry names an expert of 0 to 15; the 8 entries of a token differ; among the 32 tokens of one ep index in one layer no expert is named more than 32 times, and in some such blocks one is named exactly 32 times. `router`: entries of order 2 / sqrt(4096); all columns of a layer may share a common added vector with entries of order 50 / sqrt(4096).
All inputs are finite; a program needn't handle non-finite values.
Results may differ from a plain program's by a relative error of at most 0.02.
Values may be sent and summed in bfloat16 or wider, within the bound.
A program may use at most 64 MiB of HBM per device.

v0:
```python
import jax
import jax.numpy as jnp
from jax import lax
from jax.sharding import PartitionSpec as P

TOP = 8
LAYERS = 2
norm_eps = 1e-06


def body(tokens, norm_gains, router, w_gate, w_up, w_down, expert_ids):
    n_tp = lax.axis_size("tp")
    n_ep = lax.axis_size("ep")
    local_width = tokens.shape[1]
    full_width = local_width * n_tp
    rows_dev = tokens.shape[0]
    local_exp = w_gate.shape[1]
    experts = local_exp * n_ep
    capacity = 2 * rows_dev * TOP // experts
    current = tokens
    for layer_idx in range(LAYERS):
        gain = norm_gains[layer_idx]
        weight = router[layer_idx]
        ids = expert_ids[layer_idx]
        normed = None
        whole = lax.all_gather(current, "tp", axis=1, tiled=True)
        wide_rows = whole.astype(jnp.float32)
        square_sum = jnp.sum(wide_rows * wide_rows, axis=1)
        scaled = (wide_rows * gain[None, :]).astype(jnp.bfloat16)
        raw_logits = jnp.dot(scaled, weight, preferred_element_type=jnp.float32)
        inverse = lax.rsqrt(square_sum / full_width + norm_eps)
        normed = (scaled.astype(jnp.float32) * inverse[:, None]).astype(jnp.bfloat16)
        logits = raw_logits * inverse[:, None]
        choose = ids[:, :, None] == lax.iota(jnp.int32, experts)[None, None, :]
        picked = jnp.sum(jnp.where(choose, logits[:, None, :], 0.0), axis=-1)
        gate_probs = jax.nn.softmax(picked, axis=-1)
        onehot = choose.reshape(rows_dev * TOP, experts).astype(jnp.int32)
        earlier = jnp.cumsum(onehot, axis=0) - onehot
        slot_index = jnp.sum(earlier * onehot, axis=1).reshape(rows_dev, TOP)
        slot_key = ids * capacity + slot_index
        slot_hits = slot_key[None, :, :] == lax.iota(jnp.int32, experts * capacity)[:, None, None]
        route_matrix = jnp.any(slot_hits, axis=-1).astype(jnp.bfloat16)
        combine_matrix = jnp.sum(jnp.where(slot_hits, gate_probs[None, :, :], 0.0), axis=-1).T
        outgoing = jnp.dot(route_matrix, normed, preferred_element_type=jnp.float32).astype(
            jnp.bfloat16
        )
        outgoing = outgoing.reshape(n_ep, local_exp * capacity, full_width)
        incoming = lax.all_to_all(outgoing, "ep", split_axis=0, concat_axis=0, tiled=True)
        arrived = incoming.reshape(n_ep, local_exp, capacity, full_width).transpose(1, 0, 2, 3)
        arrived = arrived.reshape(local_exp, n_ep * capacity, full_width)
        gate_proj = jnp.einsum(
            "erd,edf->erf", arrived, w_gate[layer_idx], preferred_element_type=jnp.float32
        )
        up_proj = jnp.einsum(
            "erd,edf->erf", arrived, w_up[layer_idx], preferred_element_type=jnp.float32
        )
        inner = (jax.nn.silu(gate_proj) * up_proj).astype(jnp.bfloat16)
        down_local = w_down[layer_idx]

        def project():
            down_piece = lax.slice_in_dim(down_local, 0, local_width * lax.axis_size("tp"), axis=2)
            return jnp.einsum("erf,efd->der", inner, down_piece, preferred_element_type=jnp.float32)

        summed = lax.psum_scatter(
            project().astype(jnp.bfloat16), "tp", scatter_dimension=0, tiled=True
        ).astype(jnp.float32)
        out_rows = summed.astype(jnp.bfloat16).reshape(local_width, local_exp, n_ep, capacity)
        out_rows = out_rows.transpose(2, 1, 3, 0).reshape(n_ep, local_exp * capacity, local_width)
        returned = lax.all_to_all(out_rows, "ep", split_axis=0, concat_axis=0, tiled=True)
        returned = returned.reshape(experts * capacity, local_width).astype(jnp.float32)
        moe_out = jnp.dot(combine_matrix, returned, precision=lax.Precision.HIGHEST)
        current = (current.astype(jnp.float32) + moe_out).astype(jnp.bfloat16)
    return current


def solution(mesh):
    in_specs = (
        P("ep", "tp"),
        P(),
        P(),
        P(None, "ep", None, "tp"),
        P(None, "ep", None, "tp"),
        P(None, "ep", "tp", None),
        P(None, "ep", None),
    )
    out_specs = P("ep", "tp")
    return jax.shard_map(body, mesh=mesh, in_specs=in_specs, out_specs=out_specs, check_vma=False)
```

profile of v0, /device:TPU:0, one launch (start us, length us, event | category | flops | bytes accessed | tf_op | source)
XLA Modules:
  0.0 376.2 jit_solution(15348728780867839647)
XLA Ops:
  6.5 0.7 fusion.79
  7.5 0.6 reduce-window.14
  8.5 0.2 fusion.41
  8.8 0.9 fusion.78
  9.6 15.9 %all_gather.6 = bf16[32,4096]{1,0:T(8,128)(2,1)S(1)} all-gather(bf16[32,1024]{1,0:T(8,128)(2,1)} %param.7), channel_id=1, replica_groups=mesh['ep'=8,'tp'=4] {'tp'}, dimensions={1}, use_global_device_ids=true | all-gather | bytes 327680 | tf_op jit(solution)/shard_map/all_gather | solution.py:26
  25.7 1.3 convolution_convert_fusion.3
  27.0 52.8 %all_to_all.20 = bf16[8,64,4096]{2,1,0:T(8,128)(2,1)S(1)} all-to-all(bf16[8,64,4096]{2,1,0:T(8,128)(2,1)S(1)} %bitcast.120), channel_id=1, replica_groups=mesh['ep'=8,'tp'=4] {'ep'}, dimensions={0} | all-to-all | bytes 8388608 | tf_op jit(solution)/shard_map/all_to_all | solution.py:48
  79.8 0.5 copy.30
  80.3 2.0 copy-done
  82.3 1.5 fusion.10
  83.9 8.8 %fusion = bf16[4096,2,256]{0,2,1:T(8,128)(2,1)} fusion(bf16[2,2,192,4096]{3,2,1,0:T(8,128)(2,1)} %param.12, bf16[2,256,4096]{2,1,0:T(8,128)(2,1)} %bitcast.125, bf16[2,2,4096,192]{2,3,1,0:T(8,128)(2,1)} %param.11, f32[2,256,192]{1,2,0:T(8,128)S(1)} %fusion.10), kind=kOutput, calls=%fused_computation.4 | convolution fusion | flops 1613299712 | bytes 15073280 | tf_op jit(solution)/shard_map/erf,efd->der/dot_general | solution.py:62
  92.9 0.6 reduce-window.16
  94.1 75.1 %reduce-scatter.3.cloned.1.call-done = bf16[1024,2,256]{0,2,1:T(8,128)(2,1)} async-done(((bf16[4096,2,256]{0,2,1:T(8,128)(2,1)}), bf16[1024,2,256]{0,2,1:T(8,128)(2,1)}) %reduce-scatter.3.cloned.1.call-update) | async-done | bytes 1048592 | tf_op jit(solution)/shard_map/reduce_scatter | solution.py:64
  169.3 2.3 copy.31
  171.6 3.6 all-to-all-start.1
  175.4 0.2 fusion.40
  175.7 0.2 select_reduce_fusion.1
  175.9 14.7 %all-to-all-done.1 = bf16[8,64,1024]{2,1,0:T(8,128)(2,1)S(1)} async-done(((bf16[8,64,1024]{2,1,0:T(8,128)(2,1)}), bf16[8,64,1024]{2,1,0:T(8,128)(2,1)S(1)}, u32[]{:S(2)}, u32[]{:S(2)}) %all-to-all-start.1) | async-done | bytes 1048608 | tf_op jit(solution)/shard_map/all_to_all | solution.py:69
  190.6 0.6 fusion.30
  191.2 14.4 %all_gather.7 = bf16[32,4096]{1,0:T(8,128)(2,1)S(1)} all-gather(bf16[32,1024]{1,0:T(8,128)(2,1)S(1)} %fusion.30), channel_id=1, replica_groups=mesh['ep'=8,'tp'=4] {'tp'}, dimensions={1}, use_global_device_ids=true | all-gather | bytes 327680 | tf_op jit(solution)/shard_map/all_gather | solution.py:26
  205.8 1.3 convolution_convert_fusion.1
  207.1 51.8 %all_to_all.21 = bf16[8,64,4096]{2,1,0:T(8,128)(2,1)S(1)} all-to-all(bf16[8,64,4096]{2,1,0:T(8,128)(2,1)S(1)} %bitcast.122), channel_id=1, replica_groups=mesh['ep'=8,'tp'=4] {'ep'}, dimensions={0} | all-to-all | bytes 8388608 | tf_op jit(solution)/shard_map/all_to_all | solution.py:48
  258.9 0.5 copy.36
  259.4 2.0 copy-done.1
  261.4 1.5 fusion.5
  262.9 8.8 %fusion.1 = bf16[4096,2,256]{0,2,1:T(8,128)(2,1)} fusion(bf16[2,2,192,4096]{3,2,1,0:T(8,128)(2,1)} %param.12, bf16[2,256,4096]{2,1,0:T(8,128)(2,1)} %bitcast.127, bf16[2,2,4096,192]{2,3,1,0:T(8,128)(2,1)} %param.11, f32[2,256,192]{1,2,0:T(8,128)S(1)} %fusion.5), kind=kOutput, calls=%fused_computation.5 | convolution fusion | flops 1613299712 | bytes 15073280 | tf_op jit(solution)/shard_map/erf,efd->der/dot_general | solution.py:62
  271.7 75.0 %reduce-scatter.5.cloned.1.call-done = bf16[1024,2,256]{0,2,1:T(8,128)(2,1)} async-done(((bf16[4096,2,256]{0,2,1:T(8,128)(2,1)}), bf16[1024,2,256]{0,2,1:T(8,128)(2,1)}) %reduce-scatter.5.cloned.1.call-update) | async-done | bytes 1048592 | tf_op jit(solution)/shard_map/reduce_scatter | solution.py:64
  346.7 2.3 copy.37
  349.0 3.7 all-to-all-start.3
  353.1 0.2 select_reduce_fusion
  353.3 14.8 %all-to-all-done.3 = bf16[8,64,1024]{2,1,0:T(8,128)(2,1)S(1)} async-done(((bf16[8,64,1024]{2,1,0:T(8,128)(2,1)}), bf16[8,64,1024]{2,1,0:T(8,128)(2,1)S(1)}, u32[]{:S(2)}, u32[]{:S(2)}) %all-to-all-start.3) | async-done | bytes 1048608 | tf_op jit(solution)/shard_map/all_to_all | solution.py:69
  368.1 1.2 fusion.31
  (56 shorter events, 2.5 us)
Async XLA Ops:
  6.5 162.8 %reduce-scatter.3.cloned.1.call-start = ((), (), s32[]{:S(2)}) async-start(), calls=%async_computation.6 | async-start | bytes 5242880 | tf_op jit(solution)/shard_map/reduce_scatter | solution.py:64
  27.0 55.3 %slice-start = ((s8[6291456]{0:T(1024)(128)(4,1)}), s8[4194304]{0:T(1024)(128)(4,1)S(1)}, s32[]{:S(2)}) async-start(s8[6291456]{0:T(1024)(128)(4,1)} %bitcast.136), calls=%async_computation.8 | async-start | bytes 8388608
  79.8 2.5 slice-start.1
  80.3 2.0 copy-start
  92.6 1.3 copy-start.3
  92.6 98.0 %copy-start.2 = (bf16[32,1024]{1,0:T(8,128)(2,1)S(1)}, bf16[32,1024]{1,0:T(8,128)(2,1)}, u32[]{:S(2)}) copy-start(bf16[32,1024]{1,0:T(8,128)(2,1)} %param.7) | copy-start | bytes 196612
  171.6 19.0 %all-to-all-start.1 = ((bf16[8,64,1024]{2,1,0:T(8,128)(2,1)}), bf16[8,64,1024]{2,1,0:T(8,128)(2,1)S(1)}, u32[]{:S(2)}, u32[]{:S(2)}) async-start(bf16[8,64,1024]{2,1,0:T(8,128)(2,1)} %bitcast.16), calls=%async_computation.2 | async-start | bytes 2097152 | tf_op jit(solution)/shard_map/all_to_all | solution.py:69
  175.2 171.5 %reduce-scatter.5.cloned.1.call-start = ((), (), s32[]{:S(2)}) async-start(), calls=%async_computation.7 | async-start | bytes 5242880 | tf_op jit(solution)/shard_map/reduce_scatter | solution.py:64
  207.1 54.3 %slice-start.2 = ((s8[6291456]{0:T(1024)(128)(4,1)}), s8[4194304]{0:T(1024)(128)(4,1)S(1)}, s32[]{:S(2)}) async-start(s8[6291456]{0:T(1024)(128)(4,1)} %bitcast.138), calls=%async_computation.10 | async-start | bytes 8388608
  258.9 2.5 slice-start.3
  259.4 2.0 copy-start.1
  349.0 19.0 %all-to-all-start.3 = ((bf16[8,64,1024]{2,1,0:T(8,128)(2,1)}), bf16[8,64,1024]{2,1,0:T(8,128)(2,1)S(1)}, u32[]{:S(2)}, u32[]{:S(2)}) async-start(bf16[8,64,1024]{2,1,0:T(8,128)(2,1)} %bitcast.34), calls=%async_computation.5 | async-start | bytes 2097152 | tf_op jit(solution)/shard_map/all_to_all | solution.py:69
Sparse Core Ops, SparseCore 0:
  92.8 76.4 reduce-scatter.2
  271.8 74.8 reduce-scatter.4
where the time goes:
time: 377 us; the launch traced here: 376 us
  waiting for transfers between devices  180 us (48%)
  blocking collectives  135 us (36%)
  matrix products  25.5 us (7%)
  between operations  13.6 us (4%)
  local copies, waits for them, and re-layouts  12.3 us (3%)
  starting transfers between devices  7.32 us (2%)
    reduce_scatter x2, waiting for transfers between devices, body(): lax.psum_scatter(project().astype(jnp.bfloat16), 'tp', scatter_dimension=...  150 us
    all_to_all x2, blocking collectives, body(): lax.all_to_all(outgoing, 'ep', split_axis=0, concat_axis=0, tiled=True)  105 us
    all_gather x2, blocking collectives, body(): whole = lax.all_gather(current, 'tp', axis=1, tiled=True)  30.2 us
    all_to_all x2, waiting for transfers between devices, body(): lax.all_to_all(out_rows, 'ep', split_axis=0, concat_axis=0, tiled=True)  29.5 us
    dot_general x2, matrix products, project(): jnp.einsum('erf,efd->der', inner, down_piece, preferred_element_type=jnp....  17.6 us
  transfers between devices with their start and end apart: 4, of which 4 were waited for; matrix products, arithmetic and copies ran while one was open for 1% of the time, Pallas kernels for 0%

commit v1 on v0

--- a/solution.py
+++ b/solution.py
@@ -6,6 +6,28 @@
 TOP = 8
 LAYERS = 2
 norm_eps = 1e-06
+
+
+def in_blocks(x, dim, size):
+    before, after = (x.shape[:dim], x.shape[dim + 1 :])
+    return jnp.moveaxis(x.reshape(*before, size, -1, *after), dim, 0)
+
+
+def joined_along(blocks, dim):
+    blocks = jnp.moveaxis(blocks, 0, dim)
+    dims = blocks.shape
+    return blocks.reshape(*dims[:dim], dims[dim] * dims[dim + 1], *dims[dim + 2 :])
+
+
+def exchange_in_pairs(x, axis, split_dim, concat_dim):
+    size, index = (lax.axis_size(axis), lax.axis_index(axis))
+    pieces = in_blocks(x, split_dim, size)
+    outs = [pieces[index]]
+    for turn in range(1, size):
+        sent = pieces[index ^ turn]
+        outs.append(lax.ppermute(sent, axis, [(i, i ^ turn) for i in range(size)]))
+    pieces = jnp.stack(outs)[index ^ jnp.arange(size)]
+    return joined_along(pieces, concat_dim)
 
 
 def body(tokens, norm_gains, router, w_gate, w_up, w_down, expert_ids):
@@ -45,7 +67,7 @@
             jnp.bfloat16
         )
         outgoing = outgoing.reshape(n_ep, local_exp * capacity, full_width)
-        incoming = lax.all_to_all(outgoing, "ep", split_axis=0, concat_axis=0, tiled=True)
+        incoming = exchange_in_pairs(outgoing, "ep", 0, 0)
         arrived = incoming.reshape(n_ep, local_exp, capacity, full_width).transpose(1, 0, 2, 3)
         arrived = arrived.reshape(local_exp, n_ep * capacity, full_width)
         gate_proj = jnp.einsum(

time: 377 us -> 406 us (1.077)
  blocking collectives: 135 us -> 30.4 us
  waiting for transfers between devices: 180 us -> 269 us
  local copies, waits for them, and re-layouts: 12.3 us -> 41.1 us
  starting transfers between devices: 7.32 us -> 19 us
    all_to_all x2 -> x0, blocking collectives: 105 us -> none  [body(): lax.all_to_all(outgoing, 'ep', split_axis=0, concat_axis=0, tiled=True)]
    ppermute x0 -> x14, waiting for transfers between devices: none -> 88 us  [exchange_in_pairs(): outs.append(lax.ppermute(sent, axis, [(i, i ^ turn) for i in range(size)]))]
    ppermute x0 -> x14, starting transfers between devices: none -> 11.7 us  [exchange_in_pairs(): outs.append(lax.ppermute(sent, axis, [(i, i ^ turn) for i in range(size)]))]
    unnamed x18 -> x22, local copies, waits for them, and re-layouts: 4.13 us -> 14.2 us
    gather x0 -> x2, local copies, waits for them, and re-layouts: none -> 9.94 us  [exchange_in_pairs(): pieces = jnp.stack(outs)[index ^ jnp.arange(size)]]
    another operation x3 -> x7, local copies, waits for them, and re-layouts: 0.19 us -> 7.24 us  [the longest x2 5.34 us: body(): incoming.reshape(n_ep, local_exp, capacity, full_width)]
  transfers between devices with their start and end apart: 4 -> 18, of which waited for: 4 -> 8; matrix products, arithmetic and copies ran while one was open for 1% -> 3% of each run, Pallas kernels for 0% -> 0%
where the time goes in v1:
time: 406 us; the launch traced here: 405 us
  waiting for transfers between devices  269 us (66%)
  local copies, waits for them, and re-layouts  41.1 us (10%)
  blocking collectives  30.4 us (7%)
  matrix products  29.3 us (7%)
  starting transfers between devices  19 us (5%)
  between operations  13.6 us (3%)
    reduce_scatter x2, waiting for transfers between devices, body(): lax.psum_scatter(project().astype(jnp.bfloat16), 'tp', scatter_dimension=...  151 us
    ppermute x14, waiting for transfers between devices, exchange_in_pairs(): outs.append(lax.ppermute(sent, axis, [(i, i ^ turn) for i in range(size)]))  88 us
    all_gather x2, blocking collectives, body(): whole = lax.all_gather(current, 'tp', axis=1, tiled=True)  30.4 us
    all_to_all x2, waiting for transfers between devices, body(): lax.all_to_all(out_rows, 'ep', split_axis=0, concat_axis=0, tiled=True)  29.5 us
    dot_general x2, matrix products, project(): jnp.einsum('erf,efd->der', inner, down_piece, preferred_element_type=jnp....  17.6 us
    unnamed x22, local copies, waits for them, and re-layouts  14.2 us
    ppermute x14, starting transfers between devices, exchange_in_pairs(): outs.append(lax.ppermute(sent, axis, [(i, i ^ turn) for i in range(size)]))  11.7 us
    gather x2, local copies, waits for them, and re-layouts, exchange_in_pairs(): pieces = jnp.stack(outs)[index ^ jnp.arange(size)]  9.94 us
  transfers between devices with their start and end apart: 18, of which 8 were waited for; matrix products, arithmetic and copies ran while one was open for 3% of the time, Pallas kernels for 0%

profile of v1, /device:TPU:0, one launch (start us, length us, event | category | flops | bytes accessed | tf_op | source)
XLA Modules:
  0.0 405.2 jit_solution(17291219655644058048)
XLA Ops:
  9.6 15.9 %all_gather.6 = bf16[32,4096]{1,0:T(8,128)(2,1)S(1)} all-gather(bf16[32,1024]{1,0:T(8,128)(2,1)} %param.7), channel_id=1, replica_groups=mesh['ep'=8,'tp'=4] {'tp'}, dimensions={1}, use_global_device_ids=true | all-gather | bytes 327680 | tf_op jit(solution)/shard_map/all_gather | solution.py:48
  25.7 1.3 convolution_convert_fusion.3
  27.0 1.3 dynamic-slice_bitcast_fusion.7
  28.3 2.6 collective-permute-start.6
  32.9 1.6 collective-permute-start.1
  35.3 30.7 %collective-permute-done.1 = bf16[1,64,4096]{2,1,0:T(8,128)(2,1)S(1)} collective-permute-done((bf16[1,64,4096]{2,1,0:T(8,128)(2,1)S(1)}, bf16[1,64,4096]{2,1,0:T(8,128)(2,1)S(1)}, u32[]{:S(2)}, u32[]{:S(2)}) %collective-permute-start.1) | collective-permute-done | bytes 524320 | tf_op jit(solution)/shard_map/ppermute | solution.py:28
  67.4 12.8 %collective-permute-done.2 = bf16[1,64,4096]{2,1,0:T(8,128)(2,1)S(1)} collective-permute-done((bf16[1,64,4096]{2,1,0:T(8,128)(2,1)S(1)}, bf16[1,64,4096]{2,1,0:T(8,128)(2,1)S(1)}, u32[]{:S(2)}, u32[]{:S(2)}) %collective-permute-start.2) | collective-permute-done | bytes 524320 | tf_op jit(solution)/shard_map/ppermute | solution.py:28
  84.4 5.0 %gather_fusion = bf16[8,64,4096]{2,1,0:T(8,128)(2,1)} fusion(bf16[8,64,4096]{2,1,0:T(8,128)(2,1)} %bitcast.20, s32[1024]{0:T(1024)S(1)} %pad_clamp_fusion), kind=kCustom, calls=%fused_computation | custom fusion | bytes 8388640 | tf_op jit(solution)/shard_map/gather | solution.py:29
  89.4 2.7 copy.30
  92.1 2.0 copy-done
  94.1 3.4 fusion.10
  97.5 8.8 %fusion = bf16[4096,2,256]{0,2,1:T(8,128)(2,1)} fusion(bf16[2,2,192,4096]{3,2,1,0:T(8,128)(2,1)} %param.12, bf16[2,256,4096]{2,1,0:T(8,128)(2,1)} %bitcast.185, bf16[2,2,4096,192]{2,3,1,0:T(8,128)(2,1)} %param.11, f32[2,256,192]{1,2,0:T(8,128)S(1)} %fusion.10), kind=kOutput, calls=%fused_computation.6 | convolution fusion | flops 1613299712 | bytes 15073280 | tf_op jit(solution)/shard_map/erf,efd->der/dot_general | solution.py:84
  107.8 75.7 %reduce-scatter.3.cloned.1.call-done = bf16[1024,2,256]{0,2,1:T(8,128)(2,1)} async-done(((bf16[4096,2,256]{0,2,1:T(8,128)(2,1)}), bf16[1024,2,256]{0,2,1:T(8,128)(2,1)}) %reduce-scatter.3.cloned.1.call-update) | async-done | bytes 1048592 | tf_op jit(solution)/shard_map/reduce_scatter | solution.py:86
  183.5 2.3 copy.31
  185.8 3.7 all-to-all-start
  190.2 14.7 %all-to-all-done = bf16[8,64,1024]{2,1,0:T(8,128)(2,1)S(1)} async-done(((bf16[8,64,1024]{2,1,0:T(8,128)(2,1)}), bf16[8,64,1024]{2,1,0:T(8,128)(2,1)S(1)}, u32[]{:S(2)}, u32[]{:S(2)}) %all-to-all-start) | async-done | bytes 1048608 | tf_op jit(solution)/shard_map/all_to_all | solution.py:91
  205.5 14.5 %all_gather.7 = bf16[32,4096]{1,0:T(8,128)(2,1)S(1)} all-gather(bf16[32,1024]{1,0:T(8,128)(2,1)S(1)} %fusion.30), channel_id=1, replica_groups=mesh['ep'=8,'tp'=4] {'tp'}, dimensions={1}, use_global_device_ids=true | all-gather | bytes 327680 | tf_op jit(solution)/shard_map/all_gather | solution.py:48
  220.2 1.3 convolution_convert_fusion.1
  221.5 1.3 dynamic-slice_bitcast_fusion
  223.5 2.3 collective-permute-start.12
  228.7 31.4 %collective-permute-done.8 = bf16[1,64,4096]{2,1,0:T(8,128)(2,1)S(1)} collective-permute-done((bf16[1,64,4096]{2,1,0:T(8,128)(2,1)S(1)}, bf16[1,64,4096]{2,1,0:T(8,128)(2,1)S(1)}, u32[]{:S(2)}, u32[]{:S(2)}) %collective-permute-start.8) | collective-permute-done | bytes 524320 | tf_op jit(solution)/shard_map/ppermute | solution.py:28
  261.0 13.0 %collective-permute-done.9 = bf16[1,64,4096]{2,1,0:T(8,128)(2,1)S(1)} collective-permute-done((bf16[1,64,4096]{2,1,0:T(8,128)(2,1)S(1)}, bf16[1,64,4096]{2,1,0:T(8,128)(2,1)S(1)}, u32[]{:S(2)}, u32[]{:S(2)}) %collective-permute-start.9) | collective-permute-done | bytes 524320 | tf_op jit(solution)/shard_map/ppermute | solution.py:28
  278.2 5.0 %gather_fusion.1 = bf16[8,64,4096]{2,1,0:T(8,128)(2,1)} fusion(bf16[8,64,4096]{2,1,0:T(8,128)(2,1)} %bitcast.54, s32[1024]{0:T(1024)S(1)} %pad_clamp_fusion), kind=kCustom, calls=%fused_computation.1 | custom fusion | bytes 8388640 | tf_op jit(solution)/shard_map/gather | solution.py:29
  283.1 2.7 copy.36
  285.8 2.0 copy-done.1
  287.8 3.4 fusion.5
  291.2 8.8 %fusion.1 = bf16[4096,2,256]{0,2,1:T(8,128)(2,1)} fusion(bf16[2,2,192,4096]{3,2,1,0:T(8,128)(2,1)} %param.12, bf16[2,256,4096]{2,1,0:T(8,128)(2,1)} %bitcast.187, bf16[2,2,4096,192]{2,3,1,0:T(8,128)(2,1)} %param.11, f32[2,256,192]{1,2,0:T(8,128)S(1)} %fusion.5), kind=kOutput, calls=%fused_computation.7 | convolution fusion | flops 1613299712 | bytes 15073280 | tf_op jit(solution)/shard_map/erf,efd->der/dot_general | solution.py:84
  300.0 75.8 %reduce-scatter.5.cloned.1.call-done = bf16[1024,2,256]{0,2,1:T(8,128)(2,1)} async-done(((bf16[4096,2,256]{0,2,1:T(8,128)(2,1)}), bf16[1024,2,256]{0,2,1:T(8,128)(2,1)}) %reduce-scatter.5.cloned.1.call-update) | async-done | bytes 1048592 | tf_op jit(solution)/shard_map/reduce_scatter | solution.py:86
  375.8 2.3 copy.37
  378.1 3.6 all-to-all-start.1
  382.4 14.8 %all-to-all-done.1 = bf16[8,64,1024]{2,1,0:T(8,128)(2,1)S(1)} async-done(((bf16[8,64,1024]{2,1,0:T(8,128)(2,1)}), bf16[8,64,1024]{2,1,0:T(8,128)(2,1)S(1)}, u32[]{:S(2)}, u32[]{:S(2)}) %all-to-all-start.1) | async-done | bytes 1048608 | tf_op jit(solution)/shard_map/all_to_all | solution.py:91
  397.1 1.2 fusion.31
  (92 shorter events, 23.8 us)
Async XLA Ops:
  6.5 177.0 %reduce-scatter.3.cloned.1.call-start = ((), (), s32[]{:S(2)}) async-start(), calls=%async_computation.4 | async-start | bytes 5242880 | tf_op jit(solution)/shard_map/reduce_scatter | solution.py:86
  28.3 4.6 %collective-permute-start = (bf16[1,64,4096]{2,1,0:T(8,128)(2,1)S(1)}, bf16[1,64,4096]{2,1,0:T(8,128)(2,1)S(1)}, u32[]{:S(2)}, u32[]{:S(2)}) collective-permute-start(bf16[1,64,4096]{2,1,0:T(8,128)(2,1)S(1)} %get-tuple-element.19), channel_id=1, source_target_pairs={{0,4},{4,0},{8,12},{12,8},{16,20},{20,16},{24,28},{28,24},{1,5},{5... | collective-permute-start | bytes 1572872 | tf_op jit(solution)/shard_map/ppermute | solution.py:28
  28.3 55.2 %collective-permute-start.6 = (bf16[1,64,4096]{2,1,0:T(8,128)(2,1)S(1)}, bf16[1,64,4096]{2,1,0:T(8,128)(2,1)S(1)}, u32[]{:S(2)}, u32[]{:S(2)}) collective-permute-start(bf16[1,64,4096]{2,1,0:T(8,128)(2,1)S(1)} %get-tuple-element.13), channel_id=1, source_target_pairs={{0,28},{4,24},{8,20},{12,16},{16,12},{20,8},{24,4},{28,0},{1,29},{... | collective-permute-start | bytes 1572872 | tf_op jit(solution)/shard_map/ppermute | solution.py:28
  30.9 51.9 %collective-permute-start.5 = (bf16[1,64,4096]{2,1,0:T(8,128)(2,1)S(1)}, bf16[1,64,4096]{2,1,0:T(8,128)(2,1)S(1)}, u32[]{:S(2)}, u32[]{:S(2)}) collective-permute-start(bf16[1,64,4096]{2,1,0:T(8,128)(2,1)S(1)} %get-tuple-element.14), channel_id=1, source_target_pairs={{0,24},{4,28},{8,16},{12,20},{16,8},{20,12},{24,0},{28,4},{1,25},{... | collective-permute-start | bytes 1572872 | tf_op jit(solution)/shard_map/ppermute | solution.py:28
  31.4 50.5 %collective-permute-start.4 = (bf16[1,64,4096]{2,1,0:T(8,128)(2,1)S(1)}, bf16[1,64,4096]{2,1,0:T(8,128)(2,1)S(1)}, u32[]{:S(2)}, u32[]{:S(2)}) collective-permute-start(bf16[1,64,4096]{2,1,0:T(8,128)(2,1)S(1)} %get-tuple-element.15), channel_id=1, source_target_pairs={{0,20},{4,16},{8,28},{12,24},{16,4},{20,0},{24,12},{28,8},{1,21},{... | collective-permute-start | bytes 1572872 | tf_op jit(solution)/shard_map/ppermute | solution.py:28
  32.2 48.8 %collective-permute-start.3 = (bf16[1,64,4096]{2,1,0:T(8,128)(2,1)S(1)}, bf16[1,64,4096]{2,1,0:T(8,128)(2,1)S(1)}, u32[]{:S(2)}, u32[]{:S(2)}) collective-permute-start(bf16[1,64,4096]{2,1,0:T(8,128)(2,1)S(1)} %get-tuple-element.16), channel_id=1, source_target_pairs={{0,16},{4,20},{8,24},{12,28},{16,0},{20,4},{24,8},{28,12},{1,17},{... | collective-permute-start | bytes 1572872 | tf_op jit(solution)/shard_map/ppermute | solution.py:28
  32.9 33.1 %collective-permute-start.1 = (bf16[1,64,4096]{2,1,0:T(8,128)(2,1)S(1)}, bf16[1,64,4096]{2,1,0:T(8,128)(2,1)S(1)}, u32[]{:S(2)}, u32[]{:S(2)}) collective-permute-start(bf16[1,64,4096]{2,1,0:T(8,128)(2,1)S(1)} %get-tuple-element.18), channel_id=1, source_target_pairs={{0,8},{4,12},{8,0},{12,4},{16,24},{20,28},{24,16},{28,20},{1,9},{5... | collective-permute-start | bytes 1572872 | tf_op jit(solution)/shard_map/ppermute | solution.py:28
  66.0 14.2 %collective-permute-start.2 = (bf16[1,64,4096]{2,1,0:T(8,128)(2,1)S(1)}, bf16[1,64,4096]{2,1,0:T(8,128)(2,1)S(1)}, u32[]{:S(2)}, u32[]{:S(2)}) collective-permute-start(bf16[1,64,4096]{2,1,0:T(8,128)(2,1)S(1)} %get-tuple-element.17), channel_id=1, source_target_pairs={{0,12},{4,8},{8,4},{12,0},{16,28},{20,24},{24,20},{28,16},{1,13},{... | collective-permute-start | bytes 1572872 | tf_op jit(solution)/shard_map/ppermute | solution.py:28
  92.1 2.0 copy-start
  106.3 1.3 copy-start.3
  106.3 98.6 %copy-start.2 = (bf16[32,1024]{1,0:T(8,128)(2,1)S(1)}, bf16[32,1024]{1,0:T(8,128)(2,1)}, u32[]{:S(2)}) copy-start(bf16[32,1024]{1,0:T(8,128)(2,1)} %param.7) | copy-start | bytes 196612
  185.8 19.0 %all-to-all-start = ((bf16[8,64,1024]{2,1,0:T(8,128)(2,1)}), bf16[8,64,1024]{2,1,0:T(8,128)(2,1)S(1)}, u32[]{:S(2)}, u32[]{:S(2)}) async-start(bf16[8,64,1024]{2,1,0:T(8,128)(2,1)} %bitcast.32), calls=%async_computation.1 | async-start | bytes 2097152 | tf_op jit(solution)/shard_map/all_to_all | solution.py:91
  189.5 186.3 %reduce-scatter.5.cloned.1.call-start = ((), (), s32[]{:S(2)}) async-start(), calls=%async_computation.5 | async-start | bytes 5242880 | tf_op jit(solution)/shard_map/reduce_scatter | solution.py:86
  222.8 4.4 %collective-permute-start.7 = (bf16[1,64,4096]{2,1,0:T(8,128)(2,1)S(1)}, bf16[1,64,4096]{2,1,0:T(8,128)(2,1)S(1)}, u32[]{:S(2)}, u32[]{:S(2)}) collective-permute-start(bf16[1,64,4096]{2,1,0:T(8,128)(2,1)S(1)} %get-tuple-element.11), channel_id=1, source_target_pairs={{0,4},{4,0},{8,12},{12,8},{16,20},{20,16},{24,28},{28,24},{1,5},{5... | collective-permute-start | bytes 1572872 | tf_op jit(solution)/shard_map/ppermute | solution.py:28
  222.8 54.5 %collective-permute-start.13 = (bf16[1,64,4096]{2,1,0:T(8,128)(2,1)S(1)}, bf16[1,64,4096]{2,1,0:T(8,128)(2,1)S(1)}, u32[]{:S(2)}, u32[]{:S(2)}) collective-permute-start(bf16[1,64,4096]{2,1,0:T(8,128)(2,1)S(1)} %get-tuple-element.5), channel_id=1, source_target_pairs={{0,28},{4,24},{8,20},{12,16},{16,12},{20,8},{24,4},{28,0},{1,29},{... | collective-permute-start | bytes 1572872 | tf_op jit(solution)/shard_map/ppermute | solution.py:28
  223.5 53.0 %collective-permute-start.12 = (bf16[1,64,4096]{2,1,0:T(8,128)(2,1)S(1)}, bf16[1,64,4096]{2,1,0:T(8,128)(2,1)S(1)}, u32[]{:S(2)}, u32[]{:S(2)}) collective-permute-start(bf16[1,64,4096]{2,1,0:T(8,128)(2,1)S(1)} %get-tuple-element.6), channel_id=1, source_target_pairs={{0,24},{4,28},{8,16},{12,20},{16,8},{20,12},{24,0},{28,4},{1,25},{... | collective-permute-start | bytes 1572872 | tf_op jit(solution)/shard_map/ppermute | solution.py:28
  225.8 49.8 %collective-permute-start.11 = (bf16[1,64,4096]{2,1,0:T(8,128)(2,1)S(1)}, bf16[1,64,4096]{2,1,0:T(8,128)(2,1)S(1)}, u32[]{:S(2)}, u32[]{:S(2)}) collective-permute-start(bf16[1,64,4096]{2,1,0:T(8,128)(2,1)S(1)} %get-tuple-element.7), channel_id=1, source_target_pairs={{0,20},{4,16},{8,28},{12,24},{16,4},{20,0},{24,12},{28,8},{1,21},{... | collective-permute-start | bytes 1572872 | tf_op jit(solution)/shard_map/ppermute | solution.py:28
  226.3 48.5 %collective-permute-start.10 = (bf16[1,64,4096]{2,1,0:T(8,128)(2,1)S(1)}, bf16[1,64,4096]{2,1,0:T(8,128)(2,1)S(1)}, u32[]{:S(2)}, u32[]{:S(2)}) collective-permute-start(bf16[1,64,4096]{2,1,0:T(8,128)(2,1)S(1)} %get-tuple-element.8), channel_id=1, source_target_pairs={{0,16},{4,20},{8,24},{12,28},{16,0},{20,4},{24,8},{28,12},{1,17},{... | collective-permute-start | bytes 1572872 | tf_op jit(solution)/shard_map/ppermute | solution.py:28
  227.2 32.9 %collective-permute-start.8 = (bf16[1,64,4096]{2,1,0:T(8,128)(2,1)S(1)}, bf16[1,64,4096]{2,1,0:T(8,128)(2,1)S(1)}, u32[]{:S(2)}, u32[]{:S(2)}) collective-permute-start(bf16[1,64,4096]{2,1,0:T(8,128)(2,1)S(1)} %get-tuple-element.10), channel_id=1, source_target_pairs={{0,8},{4,12},{8,0},{12,4},{16,24},{20,28},{24,16},{28,20},{1,9},{5... | collective-permute-start | bytes 1572872 | tf_op jit(solution)/shard_map/ppermute | solution.py:28
  260.1 13.8 %collective-permute-start.9 = (bf16[1,64,4096]{2,1,0:T(8,128)(2,1)S(1)}, bf16[1,64,4096]{2,1,0:T(8,128)(2,1)S(1)}, u32[]{:S(2)}, u32[]{:S(2)}) collective-permute-start(bf16[1,64,4096]{2,1,0:T(8,128)(2,1)S(1)} %get-tuple-element.9), channel_id=1, source_target_pairs={{0,12},{4,8},{8,4},{12,0},{16,28},{20,24},{24,20},{28,16},{1,13},{... | collective-permute-start | bytes 1572872 | tf_op jit(solution)/shard_map/ppermute | solution.py:28
  285.8 2.0 copy-start.1
  378.1 19.0 %all-to-all-start.1 = ((bf16[8,64,1024]{2,1,0:T(8,128)(2,1)}), bf16[8,64,1024]{2,1,0:T(8,128)(2,1)S(1)}, u32[]{:S(2)}, u32[]{:S(2)}) async-start(bf16[8,64,1024]{2,1,0:T(8,128)(2,1)} %bitcast.65), calls=%async_computation.3 | async-start | bytes 2097152 | tf_op jit(solution)/shard_map/all_to_all | solution.py:91
Sparse Core Ops, SparseCore 0:
  106.4 77.0 reduce-scatter.2
  300.2 75.6 reduce-scatter.4
